TPU v7x, 256 devices: a whole 4x4x8 slice. The times are simulated.
256 devices in a mesh: tm: 2 (over y_lo), row: 16 (over y_hi, z), col: 8 (over x, core).
Axes of the slice: x: 4, y: 4 (y_hi: 2, y_lo: 2; y = y_hi * 2 + y_lo), z: 8, core: 2. Of those that a mesh axis runs over, the one named last changes fastest.
Arguments:
- returns: bfloat16 [272, 16384], P('tm', ('row', 'col')), may hold values from -60 to 60
- window: int32 [1], replicated, may hold values from 200 to 256
- out_days: int32 [4], replicated, may hold values from 255 to 271
Outputs:
- correlation: bfloat16 [4, 16384, 16384], P(None, 'row', ('col', 'tm'))
Inputs may be any that keep to these rules, and one draw needn't show every extreme that they name: One window length for all days. `out_days`: days may repeat.
All inputs are finite; a program needn't handle non-finite values.
Results may differ from a plain program's by a relative error of at most 0.001.
Values may be sent and summed in bfloat16 or wider, within the bound.
A program may use at most 128 MiB of HBM per device.

v0:
```python
import jax
import jax.numpy as jnp
from jax import lax
from jax.sharding import PartitionSpec as P


def moments(mask, block):
    series = block.astype(jnp.float32)
    first = jnp.dot(mask, series, precision=lax.Precision.HIGHEST)
    second = jnp.dot(mask, series * series, precision=lax.Precision.HIGHEST)
    return (first, second)


def on_device(returns, window, out_days):
    width = window[0]
    wide = width.astype(jnp.float32)
    tm_count = lax.axis_size("tm")
    tm_index = lax.axis_index("tm")
    share = lax.axis_size("row") // lax.axis_size("col")
    local = lax.all_gather(returns, "tm", axis=0, tiled=True)
    row_series = lax.all_gather(local, "col", axis=1, tiled=True)
    block_width = row_series.shape[1]
    col_index = lax.axis_index("col")
    range_width = share * block_width
    half = range_width // tm_count
    half_start = tm_index * half
    range_start = col_index * range_width
    wanted_start = range_start + half_start
    everything = lax.all_gather(row_series, "row", axis=1, tiled=True)
    col_series = lax.dynamic_slice_in_dim(everything, wanted_start, half, 1)
    day_count = local.shape[0]
    day_ids = jnp.arange(day_count, dtype=jnp.int32)
    inside = (day_ids[None, :] <= out_days[:, None]) & (
        day_ids[None, :] > out_days[:, None] - width
    )
    mask = jnp.where(inside, 1.0, 0.0).astype(jnp.float32)
    weighted = mask.astype(jnp.bfloat16)[:, :, None] * row_series[None, :, :]
    gram = jnp.einsum("kda,db->kab", weighted, col_series, preferred_element_type=jnp.float32)
    first_rows, second_rows = moments(mask, row_series)
    first_cols, second_cols = moments(mask, col_series)
    scale_rows = lax.rsqrt((second_rows - first_rows * first_rows / wide) / wide + 1e-06)
    scale_cols = lax.rsqrt((second_cols - first_cols * first_cols / wide) / wide + 1e-06)
    cov = gram - first_rows[:, :, None] * first_cols[:, None, :] / wide
    return (cov * scale_rows[:, :, None] * scale_cols[:, None, :] / wide).astype(jnp.bfloat16)


def solution(mesh):
    return jax.shard_map(
        on_device,
        mesh=mesh,
        in_specs=(P("tm", ("row", "col")), P(), P()),
        out_specs=P(None, "row", ("col", "tm")),
        check_vma=False,
    )
```

profile of v0, /device:TPU:1, one launch (start us, length us, event | category | flops | bytes accessed | tf_op | source)
XLA Modules:
  0.0 188.0 jit_solution(15276482759653825243)
XLA Ops:
  6.5 0.0 all-gather.2.cloned.1.call-start
  6.5 4.4 %all_gather.9 = bf16[272,128]{1,0:T(8,128)(2,1)S(1)} all-gather(bf16[136,128]{1,0:T(8,128)(2,1)} %param.3), channel_id=1, replica_groups=mesh['tm'=2,'row'=16,'col'=8] {'tm'}, dimensions={0}, use_global_device_ids=true | all-gather | bytes 104448 | tf_op jit(solution)/shard_map/all_gather | solution.py:20
  10.9 16.4 %all_gather.10 = bf16[272,1024]{1,0:T(8,128)(2,1)} all-gather(bf16[272,128]{1,0:T(8,128)(2,1)S(1)} %all_gather.9), channel_id=1, replica_groups=mesh['tm'=2,'row'=16,'col'=8] {'col'}, dimensions={1}, use_global_device_ids=true | all-gather | bytes 626688 | tf_op jit(solution)/shard_map/all_gather | solution.py:21
  27.3 0.0 all-gather.2.cloned.1.call-update
  28.0 0.7 broadcast_subtract_fusion
  28.7 0.7 select_convert_fusion
  29.4 1.4 fusion.41
  30.8 1.8 fusion.18
  32.7 135.3 %all-gather.2.cloned.1.call-done = bf16[272,16384]{1,0:T(8,128)(2,1)} async-done(((bf16[272,1024]{1,0:T(8,128)(2,1)}), bf16[272,16384]{1,0:T(8,128)(2,1)}) %all-gather.2.cloned.1.call-update) | async-done | bytes 8912912 | tf_op jit(solution)/shard_map/all_gather | solution.py:29
  168.0 1.4 fusion.35
  169.4 1.8 fusion.30
  171.2 9.9 %divide_convert_fusion = bf16[4,1024,1024]{2,1,0:T(8,128)(2,1)} fusion(f32[4,1024]{1,0:T(4,128)S(1)} %fusion.30, f32[4,1024]{1,0:T(4,128)S(1)} %fusion.18, f32[]{:T(128)S(6)} %convert_element_type.20, f32[4,1024]{1,0:T(4,128)S(1)} %fusion.35, f32[4,1024]{1,0:T(4,128)S(1)} %fusion.41, bf16[272,1024]{1,0:T(8,128)(2,1)} %all_gather.10, ...), kind=kOutput, calls=%fused_computation | convolution fusion | flops 2312175616 | bytes 9570440 | tf_op jit(solution)/shard_map/kda,db->kab/dot_general | solution.py:38
Async XLA Ops:
  6.5 161.4 %all-gather.2.cloned.1.call-start = ((), (), s32[]{:S(2)}) async-start(), calls=%async_computation | async-start | bytes 9469952 | tf_op jit(solution)/shard_map/all_gather | solution.py:29
Sparse Core Ops, SparseCore 0:
  27.5 140.4 all-gather.1
where the time goes:
time: 188 us
  waiting for transfers between devices  135 us (72%)
  blocking collectives  20.8 us (11%)
  matrix products  16.4 us (9%)
  between operations  14.1 us (8%)
    all_gather x1, waiting for transfers between devices, on_device(): everything = lax.all_gather(row_series, 'row', axis=1, tiled=True)  135 us
    all_gather x1, blocking collectives, on_device(): row_series = lax.all_gather(local, 'col', axis=1, tiled=True)  16.4 us
    dot_general x1, matrix products, on_device(): jnp.einsum('kda,db->kab', weighted, col_series, preferred_element_type=jn...  9.89 us
    all_gather x1, blocking collectives, on_device(): local = lax.all_gather(returns, 'tm', axis=0, tiled=True)  4.36 us
  transfers between devices with their start and end apart: 1, of which 1 were waited for; matrix products, arithmetic and copies ran while one was open for 2% of the time, Pallas kernels for 0%

commit v1 on v0

v1 whole, which is shorter than its diff:
```python
import jax
import jax.numpy as jnp
from jax import lax
from jax.experimental import pallas as pl
from jax.experimental.pallas import tpu as pltpu
from jax.sharding import PartitionSpec as P

MESH = pl.DeviceIdType.MESH
BF = jnp.bfloat16
F32 = jnp.float32
HALF = 136
WIDTH = 128
ROWS = 1024
ORDER = (1, 7, 2, 6, 3, 5, 4)


def place():
    row = lax.axis_index("row")
    col = lax.axis_index("col")
    return col // 2, row // 8, lax.axis_index("tm"), row % 8, col % 2


def device(x, y_hi, y_lo, z, core):
    return {"tm": y_lo, "row": y_hi * 8 + z, "col": x * 2 + core}


def gather_kernel(src, rows, cols, stage_sem, zs, zr, rs, rr, ys, yr, xs, xr):
    x, yh, yl, z, c = place()

    def slot_of(xd, y_lo, core):
        final = y_lo * 8 + x * 2 + core
        return jnp.where(xd == x, final, 16 + xd * 4 + y_lo * 2 + core)

    def matched(zz):
        return jnp.logical_and(zz % 2 == yl, (zz // 2) % 2 == c)

    def lies(zz):
        return jnp.where(matched(zz), slot_of(2 * yh + zz // 4, yl, c), 32 + zz)

    own = yl * 8 + x * 2 + c
    mine = lies(z)

    stages = []
    for n, (ref, at) in enumerate(((rows, own), (cols, mine))):
        first = pltpu.make_async_copy(
            src.at[pl.ds(pl.multiple_of(yl * 120, 8), 16)], ref.at[at, pl.ds(0, 16)], stage_sem.at[2 * n]
        )
        rest = pltpu.make_async_copy(
            src.at[pl.ds(pl.multiple_of(16 - yl * 16, 8), 120)], ref.at[at, pl.ds(16, 120)], stage_sem.at[2 * n + 1]
        )
        first.start()
        rest.start()
        stages += [first, rest]

    plane = [(dx, dl, dc) for dx in (0, 1, 3, 2) for dl in (0, 1) for dc in (0, 1)][1:]

    def in_plane(dx, dl, dc):
        return device((x + dx) % 4, yh, (yl + dl) % 2, z, (c + dc) % 2)

    barrier = pltpu.get_barrier_semaphore()
    partners = [in_plane(*d) for d in plane]
    partners += [device(x, yh, yl, (z + d) % 8, c) for d in ORDER]
    partners += [device(x, 1 - yh, (yl + dl) % 2, z, (c + dc) % 2) for dl in (0, 1) for dc in (0, 1)]
    for partner in partners:
        pl.semaphore_signal(barrier, inc=1, device_id=partner, device_id_type=MESH)
    for stage in stages:
        stage.wait()
    pl.semaphore_wait(barrier, len(partners))

    z_out, z_in = [], []
    for n, d in enumerate(ORDER):
        copy = pltpu.make_async_remote_copy(
            src_ref=rows.at[own],
            dst_ref=cols.at[mine],
            send_sem=zs.at[n],
            recv_sem=zr.at[n],
            device_id=device(x, yh, yl, (z + d) % 8, c),
            device_id_type=MESH,
        )
        copy.start()
        z_out.append(copy)
        z_in.append(
            pltpu.make_async_remote_copy(
                src_ref=rows.at[own],
                dst_ref=cols.at[lies((z + 8 - d) % 8)],
                send_sem=zs.at[n],
                recv_sem=zr.at[n],
                device_id=device(x, yh, yl, (z + d) % 8, c),
                device_id_type=MESH,
            )
        )

    r_out, r_in = [], []
    for n, d in enumerate(plane):
        dx, dl, dc = d
        r_out.append(
            pltpu.make_async_remote_copy(
                src_ref=rows.at[own],
                dst_ref=rows.at[own],
                send_sem=rs.at[n],
                recv_sem=rr.at[n],
                device_id=in_plane(*d),
                device_id_type=MESH,
            )
        )
        r_out[-1].start()
        from_x, from_l, from_c = (x + 4 - dx) % 4, (yl + dl) % 2, (c + dc) % 2
        r_in.append(
            pltpu.make_async_remote_copy(
                src_ref=rows.at[own],
                dst_ref=rows.at[from_l * 8 + from_x * 2 + from_c],
                send_sem=rs.at[n],
                recv_sem=rr.at[n],
                device_id=in_plane(*d),
                device_id_type=MESH,
            )
        )

    def y_copy(step, j, zz):
        xd = 2 * yh + zz // 4
        to_h = (yh + j) % 2
        to = slot_of(xd, yl, c)
        return pltpu.make_async_remote_copy(
            src_ref=cols.at[lies(zz)],
            dst_ref=cols.at[to],
            send_sem=ys.at[2 * step + j],
            recv_sem=yr.at[xd * 4 + yl * 2 + c],
            device_id=device(x, to_h, zz % 2, z, (zz // 2) % 2),
            device_id_type=MESH,
        )

    def y_send(step, zz):
        y_copy(step, 1, zz).start()

        @pl.when(jnp.logical_not(matched(zz)))
        def _():
            y_copy(step, 0, zz).start()

    def y_sent(step, zz):
        y_copy(step, 1, zz).wait_send()

        @pl.when(jnp.logical_not(matched(zz)))
        def _():
            y_copy(step, 0, zz).wait_send()

    low = c * 2 + yl
    near = (((z + 8 - low) % 8 + 2) // 4) % 2

    def y_wait(xd, y_lo, core):
        here = jnp.logical_and(xd // 2 == yh, jnp.logical_and(y_lo == yl, core == c))

        @pl.when(jnp.logical_not(here))
        def _():
            pltpu.make_async_remote_copy(
                src_ref=rows.at[own],
                dst_ref=cols.at[slot_of(xd, y_lo, core)],
                send_sem=ys.at[0],
                recv_sem=yr.at[xd * 4 + y_lo * 2 + core],
                device_id=device(x, 1 - yh, yl, z, c),
                device_id_type=MESH,
            ).wait_recv()

    def x_copy(xd, y_lo):
        return pltpu.make_async_remote_copy(
            src_ref=cols.at[pl.ds(16 + xd * 4 + y_lo * 2, 2)],
            dst_ref=cols.at[pl.ds(y_lo * 8 + x * 2, 2)],
            send_sem=xs.at[xd * 2 + y_lo],
            recv_sem=xr.at[x * 2 + y_lo],
            device_id=device(xd, yh, yl, z, c),
            device_id_type=MESH,
        )

    def x_send(which):
        for half in (0, 1):
            xd = half * 2 + which
            for y_lo in (0, 1):
                y_wait(xd, y_lo, 0)
                y_wait(xd, y_lo, 1)

                @pl.when(xd != x)
                def _():
                    x_copy(xd, y_lo).start()

    y_send(0, z)
    for n, d in enumerate(ORDER):
        z_in[n].wait_recv()
        y_send(n + 1, (z + 8 - d) % 8)
        if n == 4:
            x_send(near)
    x_send(1 - near)

    for copy in r_in:
        copy.wait_recv()
    for dx in (1, 3, 2):
        for y_lo in (0, 1):
            from_x = (x + dx) % 4
            pltpu.make_async_remote_copy(
                src_ref=cols.at[pl.ds(0, 2)],
                dst_ref=cols.at[pl.ds(y_lo * 8 + from_x * 2, 2)],
                send_sem=xs.at[0],
                recv_sem=xr.at[from_x * 2 + y_lo],
                device_id=device(from_x, yh, yl, z, c),
                device_id_type=MESH,
            ).wait_recv()
    for copy in z_out + r_out:
        copy.wait_send()
    for n, d in enumerate((0, *ORDER)):
        y_sent(n, (z + 8 - d) % 8)
    for dx in (1, 3, 2):
        for y_lo in (0, 1):
            x_copy((x + dx) % 4, y_lo).wait_send()


def gather(block):
    return pl.pallas_call(
        gather_kernel,
        out_shape=(pltpu.VMEM((16, HALF, WIDTH), BF), pltpu.VMEM((40, HALF, WIDTH), BF)),
        in_specs=[pl.BlockSpec(memory_space=pl.ANY)],
        out_specs=(pl.BlockSpec(memory_space=pltpu.VMEM),) * 2,
        scratch_shapes=[
            pltpu.SemaphoreType.DMA((4,)),
            pltpu.SemaphoreType.DMA((7,)),
            pltpu.SemaphoreType.DMA((7,)),
            pltpu.SemaphoreType.DMA((15,)),
            pltpu.SemaphoreType.DMA((15,)),
            pltpu.SemaphoreType.DMA((16,)),
            pltpu.SemaphoreType.DMA((16,)),
            pltpu.SemaphoreType.DMA((8,)),
            pltpu.SemaphoreType.DMA((8,)),
        ],
        compiler_params=pltpu.CompilerParams(collective_id=0, has_side_effects=True),
        name="gather",
    )(block)


def unpack(ref, flat, folded):
    for j in range(8):
        lanes = pl.ds(j * WIDTH, WIDTH)
        flat[0:128, lanes] = ref[j, 0:128]
        flat[128:240, lanes] = ref[8 + j, 16:128]
        flat[240:248, lanes] = ref[j, 128:136]
        flat[248:256, lanes] = ref[8 + j, 128:136]
        folded[0:16, lanes] = ref[8 + j, 0:16]


def day_of(spot):
    return jnp.where(
        spot < 128, spot, jnp.where(spot < 240, spot + 8, jnp.where(spot < 248, spot - 112, spot))
    )


def correlate_kernel(window, days, row_ref, col_ref, out, a, a_fold, at, at_fold, atk, b, b_fold, bk, tiles, sem):
    width = window[0]
    wide = width.astype(F32)

    def inside(day, k):
        last = days[k]
        return jnp.logical_and(day <= last, day > last - width)

    def picks(shape, axis, k, fold):
        spot = lax.broadcasted_iota(jnp.int32, shape, axis)
        if fold:
            hit = jnp.logical_and(spot < 16, inside(spot + 256, k))
        else:
            hit = inside(day_of(spot), k)
        return jnp.where(hit, 1.0, 0.0).astype(F32)

    def masks(places, fold):
        row = lax.broadcasted_iota(jnp.int32, (16, places), 0)
        total = jnp.zeros((16, places), F32)
        for k in range(4):
            total = jnp.where(row == k, picks((16, places), 1, k, fold), total)
        return total.astype(BF)

    main_mask = masks(256, False)
    fold_mask = masks(16, True)

    def sums(flat, folded):
        first = jnp.zeros((16, ROWS), F32)
        second = jnp.zeros((16, ROWS), F32)
        for ref, mask in ((flat, main_mask), (folded, fold_mask)):
            block = ref[...]
            first += jnp.dot(mask, block, preferred_element_type=F32)
            wide_block = block.astype(F32)
            square = wide_block * wide_block
            high = square.astype(BF)
            low = (square - high.astype(F32)).astype(BF)
            second += jnp.dot(mask, high, preferred_element_type=F32)
            second += jnp.dot(mask, low, preferred_element_type=F32)
        scale = lax.rsqrt((second - first * first / wide) / wide + 1e-06)
        return first, scale

    unpack(row_ref, a, a_fold)
    unpack(col_ref, b, b_fold)
    a_fold[16:128, :] = jnp.zeros((112, ROWS), BF)
    for j in range(8):
        lanes = pl.ds(j * WIDTH, WIDTH)
        at[lanes, 0:128] = jnp.transpose(a[0:128, lanes])
        at[lanes, 128:256] = jnp.transpose(a[128:256, lanes])
        at_fold[lanes, :] = jnp.transpose(a_fold[:, lanes])
    first_c, scale_c = sums(b, b_fold)
    first_c = first_c / wide
    scale_c = scale_c / wide
    first_r, scale_r = sums(a, a_fold.at[0:16])
    pad = jnp.zeros((96, ROWS), F32)
    turned = jnp.transpose(jnp.concatenate([first_r, scale_r, pad], axis=0))

    bk[16:256, :] = b[16:256, :]
    copies = []
    for k in range(4):
        pick = picks((16, 1), 0, k, False).astype(BF)
        pick_fold = picks((16, 1), 0, k, True).astype(BF)
        bk[0:16, :] = b[0:16, :] * pick + b_fold[...] * pick_fold
        main = picks((1, 256), 1, k, False).astype(BF)
        fold = picks((1, 128), 1, k, True).astype(BF)
        atk[:, 0:128] = at[:, 0:128] * main[:, 0:128] + at_fold[...] * fold
        atk[:, 128:256] = at[:, 128:256] * main[:, 128:256]
        for m in range(4):
            part = slice(m * 256, (m + 1) * 256)
            gram = jnp.dot(atk[part, :], bk[...], preferred_element_type=F32)
            mean = turned[part, k : k + 1] * first_c[k : k + 1, :]
            value = (gram - mean) * turned[part, 16 + k : 17 + k] * scale_c[k : k + 1, :]
            tiles[k, part, :] = value.astype(BF)
            copy = pltpu.make_async_copy(tiles.at[k, pl.ds(m * 256, 256)], out.at[k, pl.ds(m * 256, 256)], sem.at[k * 4 + m])
            copy.start()
            copies.append(copy)
    for copy in copies:
        copy.wait()


def correlate(window, out_days, row_pieces, col_pieces):
    return pl.pallas_call(
        correlate_kernel,
        out_shape=jax.ShapeDtypeStruct((4, ROWS, ROWS), BF),
        in_specs=[pl.BlockSpec(memory_space=pltpu.SMEM)] * 2 + [pl.BlockSpec(memory_space=pltpu.VMEM)] * 2,
        out_specs=pl.BlockSpec(memory_space=pl.ANY),
        scratch_shapes=[
            pltpu.VMEM((256, ROWS), BF),
            pltpu.VMEM((128, ROWS), BF),
            pltpu.VMEM((ROWS, 256), BF),
            pltpu.VMEM((ROWS, 128), BF),
            pltpu.VMEM((ROWS, 256), BF),
            pltpu.VMEM((256, ROWS), BF),
            pltpu.VMEM((16, ROWS), BF),
            pltpu.VMEM((256, ROWS), BF),
            pltpu.VMEM((4, ROWS, ROWS), BF),
            pltpu.SemaphoreType.DMA((16,)),
        ],
        compiler_params=pltpu.CompilerParams(vmem_limit_bytes=48 << 20),
        name="correlate",
    )(window, out_days, row_pieces, col_pieces)


def on_device(returns, window, out_days):
    row_pieces, col_pieces = gather(returns)
    return correlate(window, out_days, row_pieces, col_pieces)


def solution(mesh):
    return jax.shard_map(
        on_device,
        mesh=mesh,
        in_specs=(P("tm", ("row", "col")), P(), P()),
        out_specs=P(None, "row", ("col", "tm")),
        check_vma=False,
    )
```

time: 188 us -> 38.2 us (0.20)
  the two profiles are of different devices: /device:TPU:1 before, /device:TPU:25 now
where the time goes in v1:
time: 38.2 us; the launch traced here: 38 us
  Pallas kernels  36.7 us (96%)
  between operations  0.67 us (2%)
  local copies, waits for them, and re-layouts  0.65 us (2%)
    pallas_call x1, Pallas kernels, gather(): pl.pallas_call(gather_kernel, out_shape=(pltpu.VMEM((16, HALF, WIDTH), BF...  30.5 us
    pallas_call x1, Pallas kernels, correlate(): pl.pallas_call(correlate_kernel, out_shape=jax.ShapeDtypeStruct((4, ROWS,...  6.24 us

profile of v1, /device:TPU:25, one launch (start us, length us, event | category | flops | bytes accessed | tf_op | source)
XLA Modules:
  0.0 38.0 jit_solution(2424295071703601937)
XLA Ops:
  0.7 30.5 %gather.1 = (bf16[16,136,128]{2,1,0:T(8,128)(2,1)S(1)}, bf16[40,136,128]{2,1,0:T(8,128)(2,1)S(1)}) custom-call(bf16[136,128]{1,0:T(8,128)(2,1)} %src.1), custom_call_target="tpu_custom_call" | custom-call | tf_op jit(solution)/shard_map/gather/pallas_call | solution.py:215
  31.1 0.0 copy-start
  31.1 0.6 %copy-done = s32[4]{0:T(128)S(1)} copy-done((s32[4]{0:T(128)S(1)}, s32[4]{0:T(128)}, u32[]{:S(2)}) %copy-start) | copy-done | bytes 40
  31.8 6.2 %correlate.1 = bf16[4,1024,1024]{2,1,0:T(8,128)(2,1)} custom-call(s32[1]{0:T(128)S(6)} %copy.4.window, s32[4]{0:T(128)S(1)} %copy-done, bf16[16,136,128]{2,1,0:T(8,128)(2,1)S(1)} %get-tuple-element.7.row_ref, bf16[40,136,128]{2,1,0:T(8,128)(2,1)S(1)} %get-tuple-element.8.col_ref), custom_call_target="tpu_custom_call" | custom-call | tf_op jit(solution)/shard_map/correlate/pallas_call | solution.py:332
Async XLA Ops:
  31.1 0.7 %copy-start = (s32[4]{0:T(128)S(1)}, s32[4]{0:T(128)}, u32[]{:S(2)}) copy-start(s32[4]{0:T(128)} %days.1) | copy-start | bytes 52

commit v2 on v0

v2 whole, which is shorter than its diff:
```python
import jax
import jax.numpy as jnp
from jax import lax
from jax.experimental import pallas as pl
from jax.experimental.pallas import tpu as pltpu
from jax.sharding import PartitionSpec as P

MESH = pl.DeviceIdType.MESH
BF = jnp.bfloat16
F32 = jnp.float32
HALF = 136
WIDTH = 128
ROWS = 1024
NEAR = (0, 3, 1, 2)


def place():
    row = lax.axis_index("row")
    col = lax.axis_index("col")
    return col >> 1, row >> 3, lax.axis_index("tm"), row & 7, col & 1


def device(x, y_hi, y_lo, z, core):
    return {"tm": y_lo, "row": y_hi * 8 + z, "col": x * 2 + core}


def bit(value, n):
    return (value >> n) & 1


def exchange(src, buf, stage_sem, zs, zr, cs, cr, rs, rr, ds, dr, during):
    x, yh, yl, z, c = place()
    own = yl * 8 + x * 2 + c

    stages = [
        pltpu.make_async_copy(
            src.at[pl.ds(pl.multiple_of(yl * 120, 8), 16)], buf.at[own, pl.ds(0, 16)], stage_sem.at[0]
        ),
        pltpu.make_async_copy(
            src.at[pl.ds(pl.multiple_of(16 - yl * 16, 8), 120)], buf.at[own, pl.ds(16, 120)], stage_sem.at[1]
        ),
    ]
    for stage in stages:
        stage.start()

    def remote(at, to, send, recv, target):
        return pltpu.make_async_remote_copy(
            src_ref=buf.at[at],
            dst_ref=buf.at[to],
            send_sem=send,
            recv_sem=recv,
            device_id=target,
            device_id_type=MESH,
        )

    beside = 1 - 2 * c

    def relay_to(i):
        to = (z + 2 * i + c) & 7
        return device(x, (yh + bit(z, 1) + bit(to, 1)) & 1, yl, to, c)

    def relay_from(i):
        at = (z + 8 - 2 * i - c) & 7
        return at, (yh + bit(z, 1) + bit(at, 1)) & 1

    def needs(i, half, step):
        at, high = relay_from(i)
        return device(2 * high + (at >> 2), (yh + half) & 1, at & 1, (z + 8 + beside * step) & 7, bit(at, 1))

    def needed_here(i):
        at, high = relay_from(i)
        return (2 * high + (at >> 2) == x) & (at & 1 == yl) & (bit(at, 1) == c)

    wanted = 4 * (x & 1) + 2 * c + yl

    def relay_at(half, x_from, core):
        same = (z + wanted + core) & 1 == 0
        at = jnp.where(same, z, (z + 7 + 2 * core) & 7)
        return at, ((x >> 1) + bit(wanted, 1) + bit(at, 1)) & 1

    def relay_is_here(half, x_from, core):
        at, high = relay_at(half, x_from, core)
        return (at == z) & (high == yh) & (half == yl) & (x_from == x) & (core == c)

    pieces = [(half, step, core) for step in (0, 1, 3, 2) for half in (0, 1) for core in (0, 1)]

    def relay_device(half, x_from, core):
        at, high = relay_at(half, x_from, core)
        return device(x_from, high, half, at, core)

    def near_by(dx, dl, dc):
        return device((x + dx) & 3, yh, (yl + dl) & 1, z, (c + dc) & 1)

    barrier = pltpu.get_barrier_semaphore()

    def greet(target):
        pl.semaphore_signal(barrier, inc=1, device_id=target, device_id_type=MESH)

    for i in (2, 1, 3):
        at, high = relay_from(i)
        greet(device(x, high, yl, at, c))

    @pl.when(c == 1)
    def _():
        at, high = relay_from(0)
        greet(device(x, high, yl, at, c))

    for half, step, core in pieces:
        x_from = (x + step) & 3
        if step == 0:

            @pl.when(jnp.logical_not(relay_is_here(half, x_from, core)))
            def _():
                greet(relay_device(half, x_from, core))

        else:
            greet(relay_device(half, x_from, core))
    for d in ((0, 1, 0), (1, 0, 0), (3, 0, 0), (2, 0, 0), (0, 0, 1)):
        greet(near_by(*d))
    kept = sum(jnp.where(needed_here(i), 1, 0) for i in range(4))
    for stage in stages:
        stage.wait()
    pl.semaphore_wait(barrier, 3 + c + 16 - kept + 5)

    sent = []

    def send(copy, when=None):
        if when is None:
            copy.start()
        else:

            @pl.when(when)
            def _():
                copy.start()

        sent.append((copy, when))

    def relay_copy(i):
        return remote(own, 32 + i, zs.at[i], zr.at[i], relay_to(i))

    for i in NEAR:
        send(relay_copy(i), c == 1 if i == 0 else None)

    mate = (1 - yl) * 8 + x * 2 + c

    def slot(half, x_from, core):
        return half * 8 + x_from * 2 + core

    def row_copy(n, at, d):
        return remote(at, at, rs.at[n], rr.at[n], near_by(*d))

    def core_copy(n, at):
        return remote(at, at, ds.at[n], dr.at[n], near_by(0, 0, 1))

    send(row_copy(0, own, (0, 1, 0)))
    for n, dx in enumerate((1, 3, 2)):
        send(row_copy(1 + n, own, (dx, 0, 0)))
    send(core_copy(0, own))

    def forward(i):
        at = jnp.where(c == 0, own, 32) if i == 0 else 32 + i
        here = needed_here(i)
        for step in (1, 0):
            for half in (1, 0):
                copy = remote(at, 16 + own, cs.at[4 * i + 2 * half + step], cr.at[own], needs(i, half, step))
                if step or half:
                    send(copy)
                else:
                    send(copy, jnp.logical_not(here))

                    @pl.when(here)
                    def _():
                        buf[16 + own] = buf[at]

    for n, i in enumerate(NEAR):
        if i == 0:

            @pl.when(c == 1)
            def _():
                relay_copy(0).wait_recv()

        else:
            relay_copy(i).wait_recv()
        forward(i)
        if n == 0:
            row_copy(0, mate, (0, 1, 0)).wait_recv()
            for k, dx in enumerate((1, 3, 2)):
                send(row_copy(4 + k, mate, (dx, 0, 0)))
            send(core_copy(1, mate))
    for n, dx in enumerate((1, 3, 2)):
        x_from = (x + 4 - dx) & 3
        for k, half in enumerate((yl, 1 - yl)):
            at = slot(half, x_from, c)
            row_copy(1 + n + 3 * k, at, (dx, 0, 0)).wait_recv()
            send(core_copy(2 + 2 * n + k, at))
    core_copy(0, slot(yl, x, 1 - c)).wait_recv()
    core_copy(1, slot(1 - yl, x, 1 - c)).wait_recv()
    for n, dx in enumerate((1, 3, 2)):
        for k, half in enumerate((yl, 1 - yl)):
            core_copy(2 + 2 * n + k, slot(half, (x + 4 - dx) & 3, 1 - c)).wait_recv()

    during()

    for half, step, core in pieces:
        x_from = (x + step) & 3
        at = slot(half, x_from, core)
        copy = remote(own, 16 + at, cs.at[0], cr.at[at], relay_device(half, x_from, core))
        if step == 0:

            @pl.when(jnp.logical_not(relay_is_here(half, x_from, core)))
            def _():
                copy.wait_recv()

        else:
            copy.wait_recv()
    for copy, when in sent:
        if when is None:
            copy.wait_send()
        else:

            @pl.when(when)
            def _():
                copy.wait_send()


def unpack(ref, first, flat, folded):
    for j in range(8):
        lanes = pl.ds(j * WIDTH, WIDTH)
        flat[0:128, lanes] = ref[first + j, 0:128]
        flat[128:240, lanes] = ref[first + 8 + j, 16:128]
        flat[240:248, lanes] = ref[first + j, 128:136]
        flat[248:256, lanes] = ref[first + 8 + j, 128:136]
        folded[0:16, lanes] = ref[first + 8 + j, 0:16]


def picks(shape, axis, window, last, fold):
    spot = lax.broadcasted_iota(jnp.int32, shape, axis)
    if fold:
        day = jnp.where(spot < 16, spot + 256, 1 << 20)
    else:
        day = jnp.where(
            spot < 128, spot, jnp.where(spot < 240, spot + 8, jnp.where(spot < 248, spot - 112, spot))
        )
    return jnp.where((day <= last) & (day > last - window), 1.0, 0.0).astype(F32)


def sums(flat, folded, main_mask, fold_mask, wide):
    first = jnp.zeros((16, ROWS), F32)
    second = jnp.zeros((16, ROWS), F32)
    for ref, mask in ((flat, main_mask), (folded, fold_mask)):
        block = ref[...]
        first += jnp.dot(mask, block, preferred_element_type=F32)
        wide_block = block.astype(F32)
        square = wide_block * wide_block
        high = square.astype(BF)
        low = (square - high.astype(F32)).astype(BF)
        second += jnp.dot(mask, high, preferred_element_type=F32)
        second += jnp.dot(mask, low, preferred_element_type=F32)
    scale = lax.rsqrt((second - first * first / wide) / wide + 1e-06)
    return first, scale


def gather_kernel(
    src, window, days_hbm,
    buf, left, turned, masks, folds, widths,
    days, a, a_fold, at, at_fold, small_sem, *sems,
):
    get_days = pltpu.make_async_copy(days_hbm, days, small_sem.at[0])
    get_days.start()

    def during():
        get_days.wait()
        width = window[0]
        wide = width.astype(F32)
        widths[...] = jnp.full((8, WIDTH), wide, F32)
        row = lax.broadcasted_iota(jnp.int32, (16, 256), 0)
        main = jnp.zeros((16, 256), F32)
        fold = jnp.zeros((16, 256), F32)
        for k in range(4):
            main = jnp.where(row == k, picks((16, 256), 1, width, days[k], False), main)
            fold = jnp.where(row == k, picks((16, 256), 1, width, days[k], True), fold)
            folds[2 * k] = picks((16, WIDTH), 0, width, days[k], False).astype(BF)
            folds[2 * k + 1] = picks((16, WIDTH), 0, width, days[k], True).astype(BF)
        masks[0:16, :] = main.astype(BF)
        masks[16:32, :] = fold.astype(BF)

        unpack(buf, 0, a, a_fold)
        a_fold[16:128, :] = jnp.zeros((112, ROWS), BF)
        for j in range(8):
            lanes = pl.ds(j * WIDTH, WIDTH)
            at[lanes, 0:128] = jnp.transpose(a[0:128, lanes])
            at[lanes, 128:256] = jnp.transpose(a[128:256, lanes])
            at_fold[lanes, :] = jnp.transpose(a_fold[:, lanes])
        first, scale = sums(a, a_fold.at[0:16], masks[0:16, :], masks[16:32, 0:16], wide)
        pad = jnp.zeros((96, ROWS), F32)
        turned[...] = jnp.transpose(jnp.concatenate([first, scale, pad], axis=0))
        for k in range(4):
            main = picks((1, 256), 1, width, days[k], False).astype(BF)
            fold = picks((1, 128), 1, width, days[k], True).astype(BF)
            left[k, :, 0:128] = at[:, 0:128] * main[:, 0:128] + at_fold[...] * fold
            left[k, :, 128:256] = at[:, 128:256] * main[:, 128:256]

    exchange(src, buf, *sems, during)


def gather(block, window, out_days):
    vmem = pl.BlockSpec(memory_space=pltpu.VMEM)
    hbm = pl.BlockSpec(memory_space=pltpu.HBM)
    return pl.pallas_call(
        gather_kernel,
        out_shape=(
            pltpu.VMEM((36, HALF, WIDTH), BF),
            pltpu.VMEM((4, ROWS, 256), BF),
            pltpu.VMEM((ROWS, WIDTH), F32),
            pltpu.VMEM((32, 256), BF),
            pltpu.VMEM((8, 16, WIDTH), BF),
            pltpu.VMEM((8, WIDTH), F32),
        ),
        in_specs=[hbm, pl.BlockSpec(memory_space=pltpu.SMEM), hbm],
        out_specs=(vmem,) * 6,
        scratch_shapes=[
            pltpu.SMEM((4,), jnp.int32),
            pltpu.VMEM((256, ROWS), BF),
            pltpu.VMEM((128, ROWS), BF),
            pltpu.VMEM((ROWS, 256), BF),
            pltpu.VMEM((ROWS, 128), BF),
            pltpu.SemaphoreType.DMA((1,)),
        ]
        + [pltpu.SemaphoreType.DMA((n,)) for n in (2, 4, 4, 16, 16, 7, 7, 8, 8)],
        compiler_params=pltpu.CompilerParams(collective_id=0, has_side_effects=True, vmem_limit_bytes=16 << 20),
        name="gather",
    )(block, window, out_days)


def correlate_kernel(buf, left, turned, masks, folds, widths, out, b, b_fold, bk, tiles, sem):
    wide = widths[0:1, 0:1]
    unpack(buf, 16, b, b_fold)
    first, scale = sums(b, b_fold, masks[0:16, :], masks[16:32, 0:16], wide)
    first = first / wide
    scale = scale / wide
    bk[16:256, :] = b[16:256, :]
    copies = []
    for k in range(4):
        for j in range(8):
            lanes = pl.ds(j * WIDTH, WIDTH)
            bk[0:16, lanes] = b[0:16, lanes] * folds[2 * k] + b_fold[:, lanes] * folds[2 * k + 1]
        for m in range(4):
            part = slice(m * 256, (m + 1) * 256)
            gram = jnp.dot(left[k, part, :], bk[...], preferred_element_type=F32)
            mean = turned[part, k : k + 1] * first[k : k + 1, :]
            value = (gram - mean) * turned[part, 16 + k : 17 + k] * scale[k : k + 1, :]
            tiles[k, part, :] = value.astype(BF)
            copy = pltpu.make_async_copy(
                tiles.at[k, pl.ds(m * 256, 256)], out.at[k, pl.ds(m * 256, 256)], sem.at[k * 4 + m]
            )
            copy.start()
            copies.append(copy)
    for copy in copies:
        copy.wait()


def correlate(*operands):
    return pl.pallas_call(
        correlate_kernel,
        out_shape=jax.ShapeDtypeStruct((4, ROWS, ROWS), BF),
        in_specs=[pl.BlockSpec(memory_space=pltpu.VMEM)] * 6,
        out_specs=pl.BlockSpec(memory_space=pl.ANY),
        scratch_shapes=[
            pltpu.VMEM((256, ROWS), BF),
            pltpu.VMEM((16, ROWS), BF),
            pltpu.VMEM((256, ROWS), BF),
            pltpu.VMEM((4, ROWS, ROWS), BF),
            pltpu.SemaphoreType.DMA((16,)),
        ],
        compiler_params=pltpu.CompilerParams(vmem_limit_bytes=32 << 20),
        name="correlate",
    )(*operands)


def on_device(returns, window, out_days):
    returns = pltpu.with_memory_space_constraint(returns, pltpu.HBM)
    out_days = pltpu.with_memory_space_constraint(out_days, pltpu.HBM)
    return correlate(*gather(returns, window, out_days))


def solution(mesh):
    return jax.shard_map(
        on_device,
        mesh=mesh,
        in_specs=(P("tm", ("row", "col")), P(), P()),
        out_specs=P(None, "row", ("col", "tm")),
        check_vma=False,
    )
```

time: 188 us -> 31.7 us (0.17)
  waiting for transfers between devices: 135 us -> 0 us
  Pallas kernels: 0 us -> 30.9 us
  blocking collectives: 20.8 us -> 0 us
  matrix products: 16.4 us -> 0 us
  between operations: 14.1 us -> 0.66 us
    all_gather x1 -> x0, waiting for transfers between devices: 135 us -> none  [on_device(): everything = lax.all_gather(row_series, 'row', axis=1, tiled=True)]
    pallas_call x0 -> x2, Pallas kernels: none -> 30.9 us  [the longest x1 25.9 us: gather(): pl.pallas_call(gather_kernel, out_shape=(pltpu.VMEM((36, HALF, WIDTH), BF...]
    all_gather x2 -> x0, blocking collectives: 20.8 us -> none  [the longest x1 16.4 us: on_device(): row_series = lax.all_gather(local, 'col', axis=1, tiled=True)]
    dot_general x5 -> x0, matrix products: 16.4 us -> none  [the longest x1 9.89 us: on_device(): jnp.einsum('kda,db->kab', weighted, col_series, preferred_element_type=jn...]
  transfers between devices with their start and end apart: 1 -> 0, of which waited for: 1 -> 0; matrix products, arithmetic and copies ran while one was open for 2% -> 0% of each run, Pallas kernels for 0% -> 0%
where the time goes in v2:
time: 31.7 us; the launch traced here: 31.5 us
  Pallas kernels  30.9 us (97%)
  between operations  0.66 us (2%)
    pallas_call x1, Pallas kernels, gather(): pl.pallas_call(gather_kernel, out_shape=(pltpu.VMEM((36, HALF, WIDTH), BF...  25.9 us
    pallas_call x1, Pallas kernels, correlate(): pl.pallas_call(correlate_kernel, out_shape=jax.ShapeDtypeStruct((4, ROWS,...  4.94 us

profile of v2, /device:TPU:1, one launch (start us, length us, event | category | flops | bytes accessed | tf_op | source)
XLA Modules:
  0.0 31.5 jit_solution(15877964871853068832)
XLA Ops:
  0.7 25.9 %gather.1 = (bf16[36,136,128]{2,1,0:T(8,128)(2,1)S(1)}, bf16[4,1024,256]{2,1,0:T(8,128)(2,1)S(1)}, f32[1024,128]{1,0:T(8,128)S(1)}, bf16[32,256]{1,0:T(8,128)(2,...) custom-call(bf16[136,128]{1,0:T(8,128)(2,1)} %src.1, s32[1]{0:T(128)S(6)} %copy.4.window, s32[4]{0:T(128)} %days_hbm.1), custom_call_target="tpu_custom_call" | custom-call | tf_op jit(solution)/shard_map/gather/pallas_call | solution.py:309
  26.6 4.9 %correlate.1 = bf16[4,1024,1024]{2,1,0:T(8,128)(2,1)} custom-call(bf16[36,136,128]{2,1,0:T(8,128)(2,1)S(1)} %get-tuple-element.11.buf, bf16[4,1024,256]{2,1,0:T(8,128)(2,1)S(1)} %get-tuple-element.12.left, f32[1024,128]{1,0:T(8,128)S(1)} %get-tuple-element.13.turned, bf16[32,256]{1,0:T(8,128)(2,1)S(1)} %get-tuple-element.14.masks, ...), custom_call_target="tpu_custom_call" | custom-call | tf_op jit(solution)/shard_map/correlate/pallas_call | solution.py:363

commit v3 on v2

--- a/solution.py
+++ b/solution.py
@@ -138,8 +138,10 @@
     def relay_copy(i):
         return remote(own, 32 + i, zs.at[i], zr.at[i], relay_to(i))
 
-    for i in NEAR:
-        send(relay_copy(i), c == 1 if i == 0 else None)
+    urgent = ((8 - z - c) >> 1) & 3
+    for step in (0, 1, 3, 2):
+        i = (urgent + step) & 3
+        send(relay_copy(i), (i > 0) | (c == 1))
 
     mate = (1 - yl) * 8 + x * 2 + c
 
@@ -160,17 +162,24 @@
     def forward(i):
         at = jnp.where(c == 0, own, 32) if i == 0 else 32 + i
         here = needed_here(i)
-        for step in (1, 0):
-            for half in (1, 0):
-                copy = remote(at, 16 + own, cs.at[4 * i + 2 * half + step], cr.at[own], needs(i, half, step))
-                if step or half:
+        for high in (0, 1):
+            half = (yh + high) & 1
+            for step in (1, 0):
+                copy = remote(at, 16 + own, cs.at[4 * i + 2 * high + step], cr.at[own], needs(i, half, step))
+                if step:
                     send(copy)
                 else:
-                    send(copy, jnp.logical_not(here))
-
-                    @pl.when(here)
-                    def _():
-                        buf[16 + own] = buf[at]
+                    send(copy, jnp.logical_not(here & (half == 0)))
+
+        @pl.when(here)
+        def _():
+            buf[16 + own] = buf[at]
+
+    def across(half, k):
+        for n, dx in enumerate((1, 3, 2)):
+            at = slot(half, (x + 4 - dx) & 3, c)
+            row_copy(1 + n + 3 * k, at, (dx, 0, 0)).wait_recv()
+            send(core_copy(2 + 2 * n + k, at))
 
     for n, i in enumerate(NEAR):
         if i == 0:
@@ -187,12 +196,9 @@
             for k, dx in enumerate((1, 3, 2)):
                 send(row_copy(4 + k, mate, (dx, 0, 0)))
             send(core_copy(1, mate))
-    for n, dx in enumerate((1, 3, 2)):
-        x_from = (x + 4 - dx) & 3
-        for k, half in enumerate((yl, 1 - yl)):
-            at = slot(half, x_from, c)
-            row_copy(1 + n + 3 * k, at, (dx, 0, 0)).wait_recv()
-            send(core_copy(2 + 2 * n + k, at))
+        if n == 1:
+            across(yl, 0)
+    across(1 - yl, 1)
     core_copy(0, slot(yl, x, 1 - c)).wait_recv()
     core_copy(1, slot(1 - yl, x, 1 - c)).wait_recv()
     for n, dx in enumerate((1, 3, 2)):
@@ -344,14 +350,14 @@
         for j in range(8):
             lanes = pl.ds(j * WIDTH, WIDTH)
             bk[0:16, lanes] = b[0:16, lanes] * folds[2 * k] + b_fold[:, lanes] * folds[2 * k + 1]
-        for m in range(4):
-            part = slice(m * 256, (m + 1) * 256)
+        for m in range(0, ROWS, 512):
+            part = slice(m, m + 512)
             gram = jnp.dot(left[k, part, :], bk[...], preferred_element_type=F32)
             mean = turned[part, k : k + 1] * first[k : k + 1, :]
             value = (gram - mean) * turned[part, 16 + k : 17 + k] * scale[k : k + 1, :]
             tiles[k, part, :] = value.astype(BF)
             copy = pltpu.make_async_copy(
-                tiles.at[k, pl.ds(m * 256, 256)], out.at[k, pl.ds(m * 256, 256)], sem.at[k * 4 + m]
+                tiles.at[k, pl.ds(m, 512)], out.at[k, pl.ds(m, 512)], sem.at[len(copies)]
             )
             copy.start()
             copies.append(copy)

time: 31.7 us -> 31.7 us (level)
  no operation moved by 1% of the time
where the time goes in v3:
time: 31.7 us; the launch traced here: 31.5 us
  Pallas kernels  30.9 us (97%)
  between operations  0.66 us (2%)
    pallas_call x1, Pallas kernels, gather(): pl.pallas_call(gather_kernel, out_shape=(pltpu.VMEM((36, HALF, WIDTH), BF...  26 us
    pallas_call x1, Pallas kernels, correlate(): pl.pallas_call(correlate_kernel, out_shape=jax.ShapeDtypeStruct((4, ROWS,...  4.86 us

profile of v3, /device:TPU:1, one launch (start us, length us, event | category | flops | bytes accessed | tf_op | source)
XLA Modules:
  0.0 31.5 jit_solution(8694634958185492516)
XLA Ops:
  0.7 26.0 %gather.1 = (bf16[36,136,128]{2,1,0:T(8,128)(2,1)S(1)}, bf16[4,1024,256]{2,1,0:T(8,128)(2,1)S(1)}, f32[1024,128]{1,0:T(8,128)S(1)}, bf16[32,256]{1,0:T(8,128)(2,...) custom-call(bf16[136,128]{1,0:T(8,128)(2,1)} %src.1, s32[1]{0:T(128)S(6)} %copy.4.window, s32[4]{0:T(128)} %days_hbm.1), custom_call_target="tpu_custom_call" | custom-call | tf_op jit(solution)/shard_map/gather/pallas_call | solution.py:315
  26.7 4.9 %correlate.1 = bf16[4,1024,1024]{2,1,0:T(8,128)(2,1)} custom-call(bf16[36,136,128]{2,1,0:T(8,128)(2,1)S(1)} %get-tuple-element.11.buf, bf16[4,1024,256]{2,1,0:T(8,128)(2,1)S(1)} %get-tuple-element.12.left, f32[1024,128]{1,0:T(8,128)S(1)} %get-tuple-element.13.turned, bf16[32,256]{1,0:T(8,128)(2,1)S(1)} %get-tuple-element.14.masks, ...), custom_call_target="tpu_custom_call" | custom-call | tf_op jit(solution)/shard_map/correlate/pallas_call | solution.py:369

commit v4 on v3

--- a/solution.py
+++ b/solution.py
@@ -251,17 +251,17 @@
 
 
 def sums(flat, folded, main_mask, fold_mask, wide):
-    first = jnp.zeros((16, ROWS), F32)
-    second = jnp.zeros((16, ROWS), F32)
-    for ref, mask in ((flat, main_mask), (folded, fold_mask)):
-        block = ref[...]
-        first += jnp.dot(mask, block, preferred_element_type=F32)
+    inner = flat[80:256, :].astype(F32)
+    first = jnp.sum(inner, axis=0, keepdims=True)
+    second = jnp.sum(inner * inner, axis=0, keepdims=True)
+    for block, mask in ((flat[0:80, :], main_mask), (folded[...], fold_mask)):
+        first += jnp.dot(mask, block, preferred_element_type=F32)[0:8]
         wide_block = block.astype(F32)
         square = wide_block * wide_block
         high = square.astype(BF)
         low = (square - high.astype(F32)).astype(BF)
-        second += jnp.dot(mask, high, preferred_element_type=F32)
-        second += jnp.dot(mask, low, preferred_element_type=F32)
+        second += jnp.dot(mask, high, preferred_element_type=F32)[0:8]
+        second += jnp.dot(mask, low, preferred_element_type=F32)[0:8]
     scale = lax.rsqrt((second - first * first / wide) / wide + 1e-06)
     return first, scale
 
@@ -297,8 +297,8 @@
             at[lanes, 0:128] = jnp.transpose(a[0:128, lanes])
             at[lanes, 128:256] = jnp.transpose(a[128:256, lanes])
             at_fold[lanes, :] = jnp.transpose(a_fold[:, lanes])
-        first, scale = sums(a, a_fold.at[0:16], masks[0:16, :], masks[16:32, 0:16], wide)
-        pad = jnp.zeros((96, ROWS), F32)
+        first, scale = sums(a, a_fold.at[0:16], masks[0:16, 0:80], masks[16:32, 0:16], wide)
+        pad = jnp.zeros((112, ROWS), F32)
         turned[...] = jnp.transpose(jnp.concatenate([first, scale, pad], axis=0))
         for k in range(4):
             main = picks((1, 256), 1, width, days[k], False).astype(BF)
@@ -341,7 +341,7 @@
 def correlate_kernel(buf, left, turned, masks, folds, widths, out, b, b_fold, bk, tiles, sem):
     wide = widths[0:1, 0:1]
     unpack(buf, 16, b, b_fold)
-    first, scale = sums(b, b_fold, masks[0:16, :], masks[16:32, 0:16], wide)
+    first, scale = sums(b, b_fold, masks[0:16, 0:80], masks[16:32, 0:16], wide)
     first = first / wide
     scale = scale / wide
     bk[16:256, :] = b[16:256, :]
@@ -350,14 +350,14 @@
         for j in range(8):
             lanes = pl.ds(j * WIDTH, WIDTH)
             bk[0:16, lanes] = b[0:16, lanes] * folds[2 * k] + b_fold[:, lanes] * folds[2 * k + 1]
-        for m in range(0, ROWS, 512):
-            part = slice(m, m + 512)
+        for m, height in ((0, 512), (512, 512)) if k < 3 else ((0, 512), (512, 256), (768, 256)):
+            part = slice(m, m + height)
             gram = jnp.dot(left[k, part, :], bk[...], preferred_element_type=F32)
             mean = turned[part, k : k + 1] * first[k : k + 1, :]
-            value = (gram - mean) * turned[part, 16 + k : 17 + k] * scale[k : k + 1, :]
+            value = (gram - mean) * turned[part, 8 + k : 9 + k] * scale[k : k + 1, :]
             tiles[k, part, :] = value.astype(BF)
             copy = pltpu.make_async_copy(
-                tiles.at[k, pl.ds(m, 512)], out.at[k, pl.ds(m, 512)], sem.at[len(copies)]
+                tiles.at[k, pl.ds(m, height)], out.at[k, pl.ds(m, height)], sem.at[len(copies)]
             )
             copy.start()
             copies.append(copy)

time: 31.7 us -> 31.4 us (level)
  no operation moved by 1% of the time
where the time goes in v4:
time: 31.4 us; the launch traced here: 31.3 us
  Pallas kernels  30.6 us (97%)
  between operations  0.66 us (2%)
    pallas_call x1, Pallas kernels, gather(): pl.pallas_call(gather_kernel, out_shape=(pltpu.VMEM((36, HALF, WIDTH), BF...  26 us
    pallas_call x1, Pallas kernels, correlate(): pl.pallas_call(correlate_kernel, out_shape=jax.ShapeDtypeStruct((4, ROWS,...  4.6 us

profile of v4, /device:TPU:1, one launch (start us, length us, event | category | flops | bytes accessed | tf_op | source)
XLA Modules:
  0.0 31.3 jit_solution(16722210694195184534)
XLA Ops:
  0.7 26.0 %gather.1 = (bf16[36,136,128]{2,1,0:T(8,128)(2,1)S(1)}, bf16[4,1024,256]{2,1,0:T(8,128)(2,1)S(1)}, f32[1024,128]{1,0:T(8,128)S(1)}, bf16[32,256]{1,0:T(8,128)(2,...) custom-call(bf16[136,128]{1,0:T(8,128)(2,1)} %src.1, s32[1]{0:T(128)S(6)} %copy.4.window, s32[4]{0:T(128)} %days_hbm.1), custom_call_target="tpu_custom_call" | custom-call | tf_op jit(solution)/shard_map/gather/pallas_call | solution.py:315
  26.7 4.6 %correlate.1 = bf16[4,1024,1024]{2,1,0:T(8,128)(2,1)} custom-call(bf16[36,136,128]{2,1,0:T(8,128)(2,1)S(1)} %get-tuple-element.11.buf, bf16[4,1024,256]{2,1,0:T(8,128)(2,1)S(1)} %get-tuple-element.12.left, f32[1024,128]{1,0:T(8,128)S(1)} %get-tuple-element.13.turned, bf16[32,256]{1,0:T(8,128)(2,1)S(1)} %get-tuple-element.14.masks, ...), custom_call_target="tpu_custom_call" | custom-call | tf_op jit(solution)/shard_map/correlate/pallas_call | solution.py:369

commit v5 on v2

--- a/solution.py
+++ b/solution.py
@@ -245,17 +245,17 @@
 
 
 def sums(flat, folded, main_mask, fold_mask, wide):
-    first = jnp.zeros((16, ROWS), F32)
-    second = jnp.zeros((16, ROWS), F32)
-    for ref, mask in ((flat, main_mask), (folded, fold_mask)):
-        block = ref[...]
-        first += jnp.dot(mask, block, preferred_element_type=F32)
+    inner = flat[80:256, :].astype(F32)
+    first = jnp.sum(inner, axis=0, keepdims=True)
+    second = jnp.sum(inner * inner, axis=0, keepdims=True)
+    for block, mask in ((flat[0:80, :], main_mask), (folded[...], fold_mask)):
+        first += jnp.dot(mask, block, preferred_element_type=F32)[0:8]
         wide_block = block.astype(F32)
         square = wide_block * wide_block
         high = square.astype(BF)
         low = (square - high.astype(F32)).astype(BF)
-        second += jnp.dot(mask, high, preferred_element_type=F32)
-        second += jnp.dot(mask, low, preferred_element_type=F32)
+        second += jnp.dot(mask, high, preferred_element_type=F32)[0:8]
+        second += jnp.dot(mask, low, preferred_element_type=F32)[0:8]
     scale = lax.rsqrt((second - first * first / wide) / wide + 1e-06)
     return first, scale
 
@@ -291,8 +291,8 @@
             at[lanes, 0:128] = jnp.transpose(a[0:128, lanes])
             at[lanes, 128:256] = jnp.transpose(a[128:256, lanes])
             at_fold[lanes, :] = jnp.transpose(a_fold[:, lanes])
-        first, scale = sums(a, a_fold.at[0:16], masks[0:16, :], masks[16:32, 0:16], wide)
-        pad = jnp.zeros((96, ROWS), F32)
+        first, scale = sums(a, a_fold.at[0:16], masks[0:16, 0:80], masks[16:32, 0:16], wide)
+        pad = jnp.zeros((112, ROWS), F32)
         turned[...] = jnp.transpose(jnp.concatenate([first, scale, pad], axis=0))
         for k in range(4):
             main = picks((1, 256), 1, width, days[k], False).astype(BF)
@@ -335,7 +335,7 @@
 def correlate_kernel(buf, left, turned, masks, folds, widths, out, b, b_fold, bk, tiles, sem):
     wide = widths[0:1, 0:1]
     unpack(buf, 16, b, b_fold)
-    first, scale = sums(b, b_fold, masks[0:16, :], masks[16:32, 0:16], wide)
+    first, scale = sums(b, b_fold, masks[0:16, 0:80], masks[16:32, 0:16], wide)
     first = first / wide
     scale = scale / wide
     bk[16:256, :] = b[16:256, :]
@@ -344,14 +344,14 @@
         for j in range(8):
             lanes = pl.ds(j * WIDTH, WIDTH)
             bk[0:16, lanes] = b[0:16, lanes] * folds[2 * k] + b_fold[:, lanes] * folds[2 * k + 1]
-        for m in range(4):
-            part = slice(m * 256, (m + 1) * 256)
+        for m, height in ((0, 512), (512, 512)) if k < 3 else ((0, 512), (512, 256), (768, 256)):
+            part = slice(m, m + height)
             gram = jnp.dot(left[k, part, :], bk[...], preferred_element_type=F32)
             mean = turned[part, k : k + 1] * first[k : k + 1, :]
-            value = (gram - mean) * turned[part, 16 + k : 17 + k] * scale[k : k + 1, :]
+            value = (gram - mean) * turned[part, 8 + k : 9 + k] * scale[k : k + 1, :]
             tiles[k, part, :] = value.astype(BF)
             copy = pltpu.make_async_copy(
-                tiles.at[k, pl.ds(m * 256, 256)], out.at[k, pl.ds(m * 256, 256)], sem.at[k * 4 + m]
+                tiles.at[k, pl.ds(m, height)], out.at[k, pl.ds(m, height)], sem.at[len(copies)]
             )
             copy.start()
             copies.append(copy)

time: 31.7 us -> 31.3 us (0.987)
  Pallas kernels: 30.9 us -> 30.5 us
    pallas_call x1, Pallas kernels: 4.94 us -> 4.6 us  [correlate(): pl.pallas_call(correlate_kernel, out_shape=jax.ShapeDtypeStruct((4, ROWS,...]
where the time goes in v5:
time: 31.3 us; the launch traced here: 31.2 us
  Pallas kernels  30.5 us (97%)
  between operations  0.66 us (2%)
    pallas_call x1, Pallas kernels, gather(): pl.pallas_call(gather_kernel, out_shape=(pltpu.VMEM((36, HALF, WIDTH), BF...  25.9 us
    pallas_call x1, Pallas kernels, correlate(): pl.pallas_call(correlate_kernel, out_shape=jax.ShapeDtypeStruct((4, ROWS,...  4.6 us

profile of v5, /device:TPU:1, one launch (start us, length us, event | category | flops | bytes accessed | tf_op | source)
XLA Modules:
  0.0 31.2 jit_solution(9085038174198925537)
XLA Ops:
  0.7 25.9 %gather.1 = (bf16[36,136,128]{2,1,0:T(8,128)(2,1)S(1)}, bf16[4,1024,256]{2,1,0:T(8,128)(2,1)S(1)}, f32[1024,128]{1,0:T(8,128)S(1)}, bf16[32,256]{1,0:T(8,128)(2,...) custom-call(bf16[136,128]{1,0:T(8,128)(2,1)} %src.1, s32[1]{0:T(128)S(6)} %copy.4.window, s32[4]{0:T(128)} %days_hbm.1), custom_call_target="tpu_custom_call" | custom-call | tf_op jit(solution)/shard_map/gather/pallas_call | solution.py:309
  26.6 4.6 %correlate.1 = bf16[4,1024,1024]{2,1,0:T(8,128)(2,1)} custom-call(bf16[36,136,128]{2,1,0:T(8,128)(2,1)S(1)} %get-tuple-element.11.buf, bf16[4,1024,256]{2,1,0:T(8,128)(2,1)S(1)} %get-tuple-element.12.left, f32[1024,128]{1,0:T(8,128)S(1)} %get-tuple-element.13.turned, bf16[32,256]{1,0:T(8,128)(2,1)S(1)} %get-tuple-element.14.masks, ...), custom_call_target="tpu_custom_call" | custom-call | tf_op jit(solution)/shard_map/correlate/pallas_call | solution.py:363

commit v6 on v5

--- a/solution.py
+++ b/solution.py
@@ -160,8 +160,8 @@
     def forward(i):
         at = jnp.where(c == 0, own, 32) if i == 0 else 32 + i
         here = needed_here(i)
-        for step in (1, 0):
-            for half in (1, 0):
+        for half in (1, 0):
+            for step in (1, 0):
                 copy = remote(at, 16 + own, cs.at[4 * i + 2 * half + step], cr.at[own], needs(i, half, step))
                 if step or half:
                     send(copy)

time: 31.3 us -> 31.3 us (level)
  no operation moved by 1% of the time
where the time goes in v6:
time: 31.3 us; the launch traced here: 31.2 us
  Pallas kernels  30.5 us (97%)
  between operations  0.66 us (2%)
    pallas_call x1, Pallas kernels, gather(): pl.pallas_call(gather_kernel, out_shape=(pltpu.VMEM((36, HALF, WIDTH), BF...  25.9 us
    pallas_call x1, Pallas kernels, correlate(): pl.pallas_call(correlate_kernel, out_shape=jax.ShapeDtypeStruct((4, ROWS,...  4.6 us

profile of v6, /device:TPU:1, one launch (start us, length us, event | category | flops | bytes accessed | tf_op | source)
XLA Modules:
  0.0 31.2 jit_solution(7194315335557656826)
XLA Ops:
  0.7 25.9 %gather.1 = (bf16[36,136,128]{2,1,0:T(8,128)(2,1)S(1)}, bf16[4,1024,256]{2,1,0:T(8,128)(2,1)S(1)}, f32[1024,128]{1,0:T(8,128)S(1)}, bf16[32,256]{1,0:T(8,128)(2,...) custom-call(bf16[136,128]{1,0:T(8,128)(2,1)} %src.1, s32[1]{0:T(128)S(6)} %copy.4.window, s32[4]{0:T(128)} %days_hbm.1), custom_call_target="tpu_custom_call" | custom-call | tf_op jit(solution)/shard_map/gather/pallas_call | solution.py:309
  26.6 4.6 %correlate.1 = bf16[4,1024,1024]{2,1,0:T(8,128)(2,1)} custom-call(bf16[36,136,128]{2,1,0:T(8,128)(2,1)S(1)} %get-tuple-element.11.buf, bf16[4,1024,256]{2,1,0:T(8,128)(2,1)S(1)} %get-tuple-element.12.left, f32[1024,128]{1,0:T(8,128)S(1)} %get-tuple-element.13.turned, bf16[32,256]{1,0:T(8,128)(2,1)S(1)} %get-tuple-element.14.masks, ...), custom_call_target="tpu_custom_call" | custom-call | tf_op jit(solution)/shard_map/correlate/pallas_call | solution.py:363
